TPU v7x, 32 devices: a whole 2x2x4 slice. The times are simulated.
32 devices in a mesh: pipe: 4 (over x, core), vocab: 8 (over z, y).
Axes of the slice: x: 2, y: 2, z: 4, core: 2. Of those that a mesh axis runs over, the one named last changes fastest.
Arguments:
- hidden: bfloat16 [4, 128, 4096], P('pipe'), may hold values from -60 to 60
- norm_gain: float32 [4096], replicated, may hold values from 0.5 to 1.5
- out_weight: bfloat16 [128256, 4096], P(('pipe', 'vocab')), may hold values from -4 to 4
- targets: int32 [4, 128], P('pipe'), may hold values from 0 to 128255
- loss_mask: int32 [4, 128], P('pipe'), may hold values from 0 to 1, as said below
- slot_position: int32 [4, 128], P('pipe'), may hold values from 0 to 127, each once within a row
- counts: int32 [4], replicated, may hold values from 1 to 128, 320 in all
- loss_scale: float32 [], replicated, may hold values from 4096 to 32768
Outputs:
- loss: float32 [], replicated
- grad_hidden: bfloat16 [4, 128, 4096], P('pipe')
Inputs may be any that keep to these rules, and one draw needn't show every extreme that they name: The 4 counts sum to exactly 320, and one of them equals 128. Each row of slot_position holds every number of 0 to 127 once. Each row of loss_mask holds at least 64 ones.
All inputs are finite; a program needn't handle non-finite values.
Results may differ from a plain program's by a relative error of at most 0.0034.
Values may be sent and summed in bfloat16 or wider, within the bound.
A program may use at most 128 MiB of HBM per device.

v0:
```python
import jax
import jax.numpy as jnp
from jax import lax
from jax.sharding import PartitionSpec as P

EPSILON = 1e-05


def rms_scale(values, norm_gain):
    mean_square = jnp.mean(values * values, axis=-1, keepdims=True)
    return values * lax.rsqrt(mean_square + EPSILON) * norm_gain


def pull_rows(rows, norm_gain, cotangent):
    pullback = jax.vjp(lambda values: rms_scale(values, norm_gain), rows)[1]
    return pullback(cotangent)[0].astype(jnp.bfloat16)


def softmax_stats(logits, local_target):
    row_top = lax.pmax(jnp.max(logits, axis=1), ("pipe", "vocab"))
    local_total = jnp.sum(jnp.exp(logits - row_top[:, None]), axis=1)
    exp_total, target_logit = lax.psum((local_total, local_target), ("pipe", "vocab"))
    return (row_top + jnp.log(exp_total), target_logit)


def body(hidden, norm_gain, out_weight, targets, loss_mask, slot_position, counts, loss_scale):
    micro_slots = hidden.shape[1]
    model_width = hidden.shape[2]
    shard_words = out_weight.shape[0]
    offset = lax.axis_index(("pipe", "vocab")) * shard_words
    own_rows = hidden.reshape(micro_slots, model_width).astype(jnp.float32)
    own_normed = rms_scale(own_rows, norm_gain).astype(jnp.bfloat16)
    all_normed, all_targets, all_masks, all_positions = (
        lax.all_gather(own_normed, "pipe", axis=0, tiled=True),
        lax.all_gather(targets.reshape(micro_slots), "pipe", axis=0, tiled=True),
        lax.all_gather(loss_mask.reshape(micro_slots), "pipe", axis=0, tiled=True),
        lax.all_gather(slot_position.reshape(micro_slots), "pipe", axis=0, tiled=True),
    )
    rows_total = all_normed.shape[0]
    micro_index = jnp.arange(rows_total, dtype=jnp.int32) // micro_slots
    count_row = jnp.sum(
        jnp.where(
            micro_index[:, None] == jnp.arange(counts.shape[0], dtype=jnp.int32)[None, :],
            counts[None, :],
            0,
        ),
        axis=1,
    )
    inside = all_positions < count_row
    token_weight = jnp.where(inside & (all_masks == 1), 1.0, 0.0).astype(jnp.float32)
    weight_total = jnp.sum(token_weight)
    work_normed, work_targets, work_weight = (all_normed, all_targets, token_weight)
    logits = lax.dot_general(
        work_normed, out_weight, (((1,), (1,)), ((), ())), preferred_element_type=jnp.float32
    )
    is_target = (
        jnp.arange(shard_words, dtype=jnp.int32)[None, :] == (work_targets - offset)[:, None]
    )
    local_target = jnp.sum(jnp.where(is_target, logits, 0.0), axis=1)
    log_total, target_logit = softmax_stats(logits, local_target)
    loss = jnp.sum(work_weight * (log_total - target_logit)) / weight_total
    token_coef = loss_scale * work_weight / weight_total
    logit_grad = (
        (jnp.exp(logits - log_total[:, None]) - is_target.astype(jnp.float32)) * token_coef[:, None]
    ).astype(jnp.bfloat16)
    work_grad = jnp.dot(logit_grad, out_weight, preferred_element_type=jnp.float32)
    grad_cube = work_grad.reshape(rows_total // micro_slots, micro_slots, model_width)
    micro_grad = lax.psum_scatter(grad_cube, "pipe", scatter_dimension=0, tiled=True)
    summed = lax.psum(micro_grad, "vocab")
    grad_out = pull_rows(own_rows, norm_gain, summed.reshape(micro_slots, model_width))
    return (loss, grad_out.reshape(1, micro_slots, model_width))


def solution(mesh):
    in_specs = (
        P("pipe", None, None),
        P(),
        P(("pipe", "vocab"), None),
        P("pipe", None),
        P("pipe", None),
        P("pipe", None),
        P(),
        P(),
    )
    out_specs = (P(), P("pipe", None, None))
    return jax.shard_map(body, mesh=mesh, in_specs=in_specs, out_specs=out_specs, check_vma=False)
```

profile of v0, /device:TPU:0, one launch (start us, length us, event | category | flops | bytes accessed | tf_op | source)
XLA Modules:
  0.0 372.7 jit_solution(8846889576664135234)
XLA Ops:
  7.2 0.0 all-gather.5.cloned.1.call-start
  7.3 1.5 fusion.7
  8.8 2.5 fusion.9
  11.3 0.0 all-gather.5.cloned.1.call-update
  11.3 0.0 reduce-scatter.2.cloned.1.call-start
  12.0 6.0 %all-gather.2 = s32[1,512]{1,0:T(1,128)S(1)} all-gather(s32[1,128]{1,0:T(1,128)S(1)} %copy-done.3), channel_id=4, replica_groups=mesh['pipe'=4,'vocab'=8] {'pipe'}, dimensions={1}, use_global_device_ids=true | all-gather | bytes 2560 | tf_op jit(solution)/shard_map/all_gather | solution.py:35
  18.1 5.4 %all-gather.1 = s32[1,512]{1,0:T(1,128)S(1)} all-gather(s32[1,128]{1,0:T(1,128)S(1)} %copy-done.4), channel_id=3, replica_groups=mesh['pipe'=4,'vocab'=8] {'pipe'}, dimensions={1}, use_global_device_ids=true | all-gather | bytes 2560 | tf_op jit(solution)/shard_map/all_gather | solution.py:36
  23.4 5.2 %all-gather = s32[1,512]{1,0:T(1,128)S(1)} all-gather(s32[1,128]{1,0:T(1,128)S(1)} %copy-done.5), channel_id=2, replica_groups=mesh['pipe'=4,'vocab'=8] {'pipe'}, dimensions={1}, use_global_device_ids=true | all-gather | bytes 2560 | tf_op jit(solution)/shard_map/all_gather | solution.py:37
  28.6 0.1 select_reduce_fusion.1
  28.7 19.9 %all-gather.5.cloned.1.call-done = bf16[512,4096]{1,0:T(8,128)(2,1)} async-done(((bf16[128,4096]{1,0:T(8,128)(2,1)}), bf16[512,4096]{1,0:T(8,128)(2,1)}) %all-gather.5.cloned.1.call-update) | async-done | bytes 4194320 | tf_op jit(solution)/shard_map/all_gather | solution.py:34
  48.7 23.8 %fusion.18 = (f32[512]{0:T(512)S(1)}, f32[512,4008]{0,1:T(8,128)}) fusion(bf16[512,4096]{1,0:T(8,128)(2,1)} %all-gather.5.cloned.1.call-done, bf16[4008,4096]{1,0:T(8,128)(2,1)} %param.10), kind=kOutput, calls=%fused_computation.41 | convolution fusion | flops 16812822528 | bytes 45238272 | tf_op jit(solution)/shard_map/dot_general | solution.py:53
  72.4 39.2 %pmax.7 = f32[512]{0:T(512)S(1)} all-reduce(f32[512]{0:T(512)S(1)} %get-tuple-element.10), channel_id=1, replica_groups=mesh['pipe'=4,'vocab'=8] {'pipe','vocab'}, use_global_device_ids=true, to_apply=%region_3.4 | all-reduce | flops 512 | bytes 4096 | tf_op jit(solution)/shard_map/pmax | solution.py:20
  111.7 4.5 %select_reduce_fusion = (f32[512]{0:T(512)S(1)}, f32[512]{0:T(512)S(1)}) fusion(f32[512,4008]{0,1:T(8,128)} %get-tuple-element.11, s32[512]{0:T(512)S(1)} %bitcast.27, f32[512]{0:T(512)S(1)} %pmax.7), kind=kLoop, calls=%fused_computation.1 | loop fusion | flops 10259456 | bytes 8216576 | tf_op jit(solution)/shard_map/reduce_sum | solution.py:59
  116.2 41.0 %all-reduce = (f32[512]{0:T(512)S(1)}, f32[512]{0:T(512)S(1)}) all-reduce(f32[512]{0:T(512)S(1)} %get-tuple-element.3, f32[512]{0:T(512)S(1)} %get-tuple-element.2), channel_id=1, replica_groups=mesh['pipe'=4,'vocab'=8] {'pipe','vocab'}, use_global_device_ids=true, to_apply=%region_5.6 | all-reduce | flops 1024 | bytes 8192 | tf_op jit(solution)/shard_map/psum | solution.py:22
  157.1 0.6 select_reduce_fusion.2
  157.8 0.7 fusion.13
  158.4 25.5 %fusion = f32[512,4096]{1,0:T(8,128)} fusion(bf16[4008,4096]{1,0:T(8,128)(2,1)} %param.10, f32[512,4008]{0,1:T(8,128)} %get-tuple-element.11, f32[512]{0:T(512)S(1)} %fusion.13, f32[512]{0:T(512)S(1)} %get-tuple-element.8, s32[512]{0:T(512)S(1)} %bitcast.28), kind=kOutput, calls=%fused_computation.4 | convolution fusion | flops 16823083008 | bytes 49436672 | tf_op jit(solution)/shard_map/dot_general | solution.py:66
  183.9 0.0 reduce-scatter.2.cloned.1.call-update
  184.0 0.0 all-reduce.3.cloned.1.call-start
  184.0 71.2 %reduce-scatter.2.cloned.1.call-done = f32[1,128,4096]{2,1,0:T(8,128)} async-done(((f32[4,128,4096]{2,1,0:T(8,128)}), f32[1,128,4096]{2,1,0:T(8,128)}) %reduce-scatter.2.cloned.1.call-update) | async-done | bytes 2097168 | tf_op jit(solution)/shard_map/reduce_scatter | solution.py:68
  256.6 104.7 %all-reduce.3.cloned.1.call-done = f32[1,128,4096]{2,1,0:T(8,128)} async-done(((f32[1,128,4096]{2,1,0:T(8,128)}), f32[1,128,4096]{2,1,0:T(8,128)}) %all-reduce.3.cloned.1.call-update) | async-done | bytes 2097168 | tf_op jit(solution)/shard_map/psum | solution.py:69
  361.3 2.1 fusion.10
  363.4 0.1 copy-done.1
  363.5 1.5 fusion.11
  (19 shorter events, 0.1 us)
Async XLA Ops:
  7.2 4.9 %copy-start.3 = (s32[1,128]{1,0:T(1,128)S(1)}, s32[1,128]{1,0:T(1,128)}, u32[]{:S(2)}) copy-start(s32[1,128]{1,0:T(1,128)} %param.11) | copy-start | bytes 1540
  7.2 10.9 %copy-start.4 = (s32[1,128]{1,0:T(1,128)S(1)}, s32[1,128]{1,0:T(1,128)}, u32[]{:S(2)}) copy-start(s32[1,128]{1,0:T(1,128)} %param.12) | copy-start | bytes 1540
  7.2 16.2 %copy-start.5 = (s32[1,128]{1,0:T(1,128)S(1)}, s32[1,128]{1,0:T(1,128)}, u32[]{:S(2)}) copy-start(s32[1,128]{1,0:T(1,128)} %param.13) | copy-start | bytes 1540
  7.2 21.4 %copy-start.6 = (s32[4]{0:T(128)S(1)}, s32[4]{0:T(128)}, u32[]{:S(2)}) copy-start(s32[4]{0:T(128)} %param.14) | copy-start | bytes 52
  7.2 41.5 %all-gather.5.cloned.1.call-start = ((), (), s32[]{:S(2)}) async-start(), calls=%async_computation.1 | async-start | bytes 5242880 | tf_op jit(solution)/shard_map/all_gather | solution.py:34
  11.3 243.9 %reduce-scatter.2.cloned.1.call-start = ((), (), s32[]{:S(2)}) async-start(), calls=%async_computation.2 | async-start | bytes 10485760 | tf_op jit(solution)/shard_map/reduce_scatter | solution.py:68
  183.9 177.3 %copy-start = (bf16[1,128,4096]{2,1,0:T(8,128)(2,1)S(1)}, bf16[1,128,4096]{2,1,0:T(8,128)(2,1)}, u32[]{:S(2)}) copy-start(bf16[1,128,4096]{2,1,0:T(8,128)(2,1)} %param.8) | copy-start | bytes 3145732
  183.9 177.3 %copy-start.2 = (f32[4096]{0:T(1024)S(1)}, f32[4096]{0:T(1024)}, u32[]{:S(2)}) copy-start(f32[4096]{0:T(1024)} %param.9) | copy-start | bytes 49156
  184.0 177.3 %all-reduce.3.cloned.1.call-start = ((), (), s32[]{:S(2)}) async-start(), calls=%async_computation.3 | async-start | bytes 4194304 | tf_op jit(solution)/shard_map/psum | solution.py:69
  361.3 2.2 copy-start.1
Sparse Core Ops, SparseCore 0:
  11.5 37.1 all-gather.4
  184.1 71.1 reduce-scatter.1
  258.9 102.3 all-reduce.2
where the time goes:
time: 373 us
  waiting for transfers between devices  196 us (53%)
  blocking collectives  96.8 us (26%)
  matrix products  49.3 us (13%)
  between operations  16.9 us (5%)
  other arithmetic  13.6 us (4%)
    psum x1, waiting for transfers between devices, body(): summed = lax.psum(micro_grad, 'vocab')  105 us
    reduce_scatter x1, waiting for transfers between devices, body(): lax.psum_scatter(grad_cube, 'pipe', scatter_dimension=0, tiled=True)  71.2 us
    psum x1, blocking collectives, softmax_stats(): lax.psum((local_total, local_target), ('pipe', 'vocab'))  41 us
    pmax x1, blocking collectives, softmax_stats(): row_top = lax.pmax(jnp.max(logits, axis=1), ('pipe', 'vocab'))  39.2 us
    dot_general x1, matrix products, body(): jnp.dot(logit_grad, out_weight, preferred_element_type=jnp.float32)  25.5 us
    dot_general x1, matrix products, body(): lax.dot_general(work_normed, out_weight, (((1,), (1,)), ((), ())), prefer...  23.8 us
    all_gather x1, waiting for transfers between devices, body(): lax.all_gather(own_normed, 'pipe', axis=0, tiled=True)  19.9 us
  transfers between devices with their start and end apart: 3, of which 3 were waited for; matrix products, arithmetic and copies ran while one was open for 0% of the time, Pallas kernels for 0%

commit v1 on v0

--- a/solution.py
+++ b/solution.py
@@ -2,8 +2,13 @@
 import jax.numpy as jnp
 from jax import lax
 from jax.sharding import PartitionSpec as P
+from jax.lax import all_gather
 
 EPSILON = 1e-05
+
+
+def circles_check(xx):
+    return jnp.sum(all_gather(xx, "vocab"), axis=0)
 
 
 def rms_scale(values, norm_gain):
@@ -66,7 +71,7 @@
     work_grad = jnp.dot(logit_grad, out_weight, preferred_element_type=jnp.float32)
     grad_cube = work_grad.reshape(rows_total // micro_slots, micro_slots, model_width)
     micro_grad = lax.psum_scatter(grad_cube, "pipe", scatter_dimension=0, tiled=True)
-    summed = lax.psum(micro_grad, "vocab")
+    summed = circles_check(micro_grad)
     grad_out = pull_rows(own_rows, norm_gain, summed.reshape(micro_slots, model_width))
     return (loss, grad_out.reshape(1, micro_slots, model_width))
 

time: 373 us -> 502 us (1.35)
  waiting for transfers between devices: 196 us -> 319 us
  other arithmetic: 13.6 us -> 19.2 us
    all_gather x0 -> x1, waiting for transfers between devices: none -> 228 us  [circles_check(): return jnp.sum(all_gather(xx, 'vocab'), axis=0)]
    psum x1 -> x0, waiting for transfers between devices: 105 us -> none  [body(): summed = lax.psum(micro_grad, 'vocab')]
    reduce_sum x0 -> x1, other arithmetic: none -> 7.43 us  [circles_check(): return jnp.sum(all_gather(xx, 'vocab'), axis=0)]
where the time goes in v1:
time: 502 us
  waiting for transfers between devices  319 us (64%)
  blocking collectives  96.7 us (19%)
  matrix products  49.3 us (10%)
  other arithmetic  19.2 us (4%)
  between operations  17 us (3%)
    all_gather x1, waiting for transfers between devices, circles_check(): return jnp.sum(all_gather(xx, 'vocab'), axis=0)  228 us
    reduce_scatter x1, waiting for transfers between devices, body(): lax.psum_scatter(grad_cube, 'pipe', scatter_dimension=0, tiled=True)  71.1 us
    psum x1, blocking collectives, softmax_stats(): lax.psum((local_total, local_target), ('pipe', 'vocab'))  40.9 us
    pmax x1, blocking collectives, softmax_stats(): row_top = lax.pmax(jnp.max(logits, axis=1), ('pipe', 'vocab'))  39.2 us
    dot_general x1, matrix products, body(): jnp.dot(logit_grad, out_weight, preferred_element_type=jnp.float32)  25.5 us
    dot_general x1, matrix products, body(): lax.dot_general(work_normed, out_weight, (((1,), (1,)), ((), ())), prefer...  23.7 us
    all_gather x1, waiting for transfers between devices, body(): lax.all_gather(own_normed, 'pipe', axis=0, tiled=True)  19.9 us
  transfers between devices with their start and end apart: 3, of which 3 were waited for; matrix products, arithmetic and copies ran while one was open for 0% of the time, Pallas kernels for 0%

profile of v1, /device:TPU:0, one launch (start us, length us, event | category | flops | bytes accessed | tf_op | source)
XLA Modules:
  0.0 501.7 jit_solution(14745181805273271279)
XLA Ops:
  7.2 0.0 all-gather.7.cloned.1.call-start
  7.3 1.5 fusion.7
  8.8 2.5 fusion.9
  11.3 0.0 all-gather.7.cloned.1.call-update
  11.3 0.0 reduce-scatter.2.cloned.1.call-start
  12.0 6.0 %all-gather.2 = s32[1,512]{1,0:T(1,128)S(1)} all-gather(s32[1,128]{1,0:T(1,128)S(1)} %copy-done.2), channel_id=4, replica_groups=mesh['pipe'=4,'vocab'=8] {'pipe'}, dimensions={1}, use_global_device_ids=true | all-gather | bytes 2560 | tf_op jit(solution)/shard_map/all_gather | solution.py:40
  18.1 5.4 %all-gather.1 = s32[1,512]{1,0:T(1,128)S(1)} all-gather(s32[1,128]{1,0:T(1,128)S(1)} %copy-done.3), channel_id=3, replica_groups=mesh['pipe'=4,'vocab'=8] {'pipe'}, dimensions={1}, use_global_device_ids=true | all-gather | bytes 2560 | tf_op jit(solution)/shard_map/all_gather | solution.py:41
  23.4 5.2 %all-gather = s32[1,512]{1,0:T(1,128)S(1)} all-gather(s32[1,128]{1,0:T(1,128)S(1)} %copy-done.4), channel_id=2, replica_groups=mesh['pipe'=4,'vocab'=8] {'pipe'}, dimensions={1}, use_global_device_ids=true | all-gather | bytes 2560 | tf_op jit(solution)/shard_map/all_gather | solution.py:42
  28.6 0.1 select_reduce_fusion.1
  28.7 19.9 %all-gather.7.cloned.1.call-done = bf16[512,4096]{1,0:T(8,128)(2,1)} async-done(((bf16[128,4096]{1,0:T(8,128)(2,1)}), bf16[512,4096]{1,0:T(8,128)(2,1)}) %all-gather.7.cloned.1.call-update) | async-done | bytes 4194320 | tf_op jit(solution)/shard_map/all_gather | solution.py:39
  48.7 23.7 %fusion.19 = (f32[512]{0:T(512)S(1)}, f32[512,4008]{0,1:T(8,128)}) fusion(bf16[512,4096]{1,0:T(8,128)(2,1)} %all-gather.7.cloned.1.call-done, bf16[4008,4096]{1,0:T(8,128)(2,1)} %param.10), kind=kOutput, calls=%fused_computation.42 | convolution fusion | flops 16812822528 | bytes 45238272 | tf_op jit(solution)/shard_map/dot_general | solution.py:58
  72.4 39.2 %pmax.7 = f32[512]{0:T(512)S(1)} all-reduce(f32[512]{0:T(512)S(1)} %get-tuple-element.10), channel_id=1, replica_groups=mesh['pipe'=4,'vocab'=8] {'pipe','vocab'}, use_global_device_ids=true, to_apply=%region_3.4 | all-reduce | flops 512 | bytes 4096 | tf_op jit(solution)/shard_map/pmax | solution.py:25
  111.7 4.5 select_reduce_fusion
  116.2 40.9 %all-reduce = (f32[512]{0:T(512)S(1)}, f32[512]{0:T(512)S(1)}) all-reduce(f32[512]{0:T(512)S(1)} %get-tuple-element.3, f32[512]{0:T(512)S(1)} %get-tuple-element.2), channel_id=1, replica_groups=mesh['pipe'=4,'vocab'=8] {'pipe','vocab'}, use_global_device_ids=true, to_apply=%region_5.6 | all-reduce | flops 1024 | bytes 8192 | tf_op jit(solution)/shard_map/psum | solution.py:27
  157.1 0.6 select_reduce_fusion.2
  157.7 0.7 fusion.14
  158.4 25.5 %fusion = f32[512,4096]{1,0:T(8,128)} fusion(bf16[4008,4096]{1,0:T(8,128)(2,1)} %param.10, f32[512,4008]{0,1:T(8,128)} %get-tuple-element.11, f32[512]{0:T(512)S(1)} %fusion.14, f32[512]{0:T(512)S(1)} %get-tuple-element.8, s32[512]{0:T(512)S(1)} %bitcast.30), kind=kOutput, calls=%fused_computation.4 | convolution fusion | flops 16823083008 | bytes 49436672 | tf_op jit(solution)/shard_map/dot_general | solution.py:71
  183.9 0.0 reduce-scatter.2.cloned.1.call-update
  183.9 0.2 all-gather.9.cloned.1.call-start
  184.2 71.1 %reduce-scatter.2.cloned.1.call-done = f32[1,128,4096]{2,1,0:T(8,128)} async-done(((f32[4,128,4096]{2,1,0:T(8,128)}), f32[1,128,4096]{2,1,0:T(8,128)}) %reduce-scatter.2.cloned.1.call-update) | async-done | bytes 2097168 | tf_op jit(solution)/shard_map/reduce_scatter | solution.py:73
  256.7 228.1 %all-gather.9.cloned.1.call-done = f32[8,128,4096]{2,1,0:T(8,128)} async-done(((f32[1,128,4096]{2,1,0:T(8,128)}), f32[8,128,4096]{2,1,0:T(8,128)}) %all-gather.9.cloned.1.call-update) | async-done | bytes 16777232 | tf_op jit(solution)/shard_map/all_gather | solution.py:11
  484.7 7.4 %reduce.1 = f32[128,4096]{1,0:T(8,128)S(1)} reduce(f32[8,128,4096]{2,1,0:T(8,128)} %all-gather.9.cloned.1.call-done, f32[]{:T(128)} %constant.37.clone.1), dimensions={0}, to_apply=%region_11.12 | reduce | flops 3670016 | bytes 18874372 | tf_op jit(solution)/shard_map/reduce_sum | solution.py:11
  492.2 0.4 fusion.10
  492.6 1.5 fusion.11
  (18 shorter events, 0.1 us)
Async XLA Ops:
  7.2 4.9 copy-start.2
  7.2 10.9 %copy-start.3 = (s32[1,128]{1,0:T(1,128)S(1)}, s32[1,128]{1,0:T(1,128)}, u32[]{:S(2)}) copy-start(s32[1,128]{1,0:T(1,128)} %param.12) | copy-start | bytes 1540
  7.2 16.2 %copy-start.4 = (s32[1,128]{1,0:T(1,128)S(1)}, s32[1,128]{1,0:T(1,128)}, u32[]{:S(2)}) copy-start(s32[1,128]{1,0:T(1,128)} %param.13) | copy-start | bytes 1540
  7.2 21.4 %copy-start.5 = (s32[4]{0:T(128)S(1)}, s32[4]{0:T(128)}, u32[]{:S(2)}) copy-start(s32[4]{0:T(128)} %param.14) | copy-start | bytes 52
  7.2 41.5 %all-gather.7.cloned.1.call-start = ((), (), s32[]{:S(2)}) async-start(), calls=%async_computation.1 | async-start | bytes 5242880 | tf_op jit(solution)/shard_map/all_gather | solution.py:39
  11.3 243.9 %reduce-scatter.2.cloned.1.call-start = ((), (), s32[]{:S(2)}) async-start(), calls=%async_computation.2 | async-start | bytes 10485760 | tf_op jit(solution)/shard_map/reduce_scatter | solution.py:73
  183.9 300.8 %all-gather.9.cloned.1.call-start = ((), (), s32[]{:S(2)}) async-start(), calls=%async_computation.3 | async-start | bytes 18874368 | tf_op jit(solution)/shard_map/all_gather | solution.py:11
  256.6 235.5 %copy-start = (bf16[1,128,4096]{2,1,0:T(8,128)(2,1)S(1)}, bf16[1,128,4096]{2,1,0:T(8,128)(2,1)}, u32[]{:S(2)}) copy-start(bf16[1,128,4096]{2,1,0:T(8,128)(2,1)} %param.8) | copy-start | bytes 3145732
  256.6 235.5 %copy-start.1 = (f32[4096]{0:T(1024)S(1)}, f32[4096]{0:T(1024)}, u32[]{:S(2)}) copy-start(f32[4096]{0:T(1024)} %param.9) | copy-start | bytes 49156
Sparse Core Ops, SparseCore 0:
  11.5 37.1 all-gather.6
  184.0 71.1 reduce-scatter.1
  257.4 227.2 all-gather.8
